TPU v7x, 128 devices: a whole 4x4x4 slice. The times are simulated.
128 devices in a mesh: chan: 16 (over x_lo, z, core), band: 8 (over y, x_hi).
Axes of the slice: x: 4 (x_hi: 2, x_lo: 2; x = x_hi * 2 + x_lo), y: 4, z: 4, core: 2. Of those that a mesh axis runs over, the one named last changes fastest.
Arguments:
- residual: float32 [128, 192, 16384], P('chan', 'band'), may hold values from -60 to 60
- weight_index: int32 [128], P('chan'), may hold values from 0 to 15
- weight_table: float32 [16], replicated, may hold values from 0.2 to 5
- gridded: float32 [2, 16, 256, 16384], P(None, 'chan', 'band'), may hold values from -6 to 6
Outputs:
- components: float32 [3, 192, 16384], P(None, 'band', 'chan')
- spectrum: float32 [2, 16, 16384, 256], P(None, 'chan', 'band')
All inputs are finite; a program needn't handle non-finite values.
Results may differ from a plain program's by a relative error of at most 0.0002.
Values sent between devices are 32-bit elements; how exact they have to be, the bound alone decides.
A program may use at most 128 MiB of HBM per device.

v0:
```python
import functools

import jax
import jax.numpy as jnp
import numpy as np
from jax import lax
from jax.experimental import pallas as pl
from jax.experimental.pallas import tpu as pltpu
from jax.sharding import PartitionSpec as P

MESH = pl.DeviceIdType.MESH
RADIX = 128
TERMS = 3
SHIFTS = (2, 1, 3, 0)


def tables():
    step = np.arange(RADIX)
    angle = 2.0 * np.pi * (np.outer(step, step) % RADIX) / RADIX
    cos, sin = (np.cos(angle), np.sin(angle))
    whole = np.block([[cos, sin], [-sin, cos]]).astype(np.float32)
    high = whole.astype(jnp.bfloat16)
    low = (whole - high.astype(np.float32)).astype(jnp.bfloat16)
    turn = 2.0 * np.pi * np.outer(step, step) / (RADIX * RADIX)
    twist_re = np.tile(np.cos(turn) / RADIX, (1, 2)).astype(np.float32)
    twist_im = np.tile(-np.sin(turn) / RADIX, (1, 2)).astype(np.float32)
    return (high, low, twist_re, twist_im)


def split_pair(value):
    high = value.astype(jnp.bfloat16)
    low = (value - high.astype(jnp.float32)).astype(jnp.bfloat16)
    return (high, low)


def three_products(high, low, value, dims):
    value_high, value_low = split_pair(value)
    mul = functools.partial(
        lax.dot_general, dimension_numbers=(dims, ((), ())), preferred_element_type=jnp.float32
    )
    return mul(high, value_high) + mul(high, value_low) + mul(low, value_high)


def solve_rows(moment, taylor):
    m0, m1, m2, m3, m4 = moment
    aa = m2 * m4 - m3 * m3
    ab = m2 * m3 - m1 * m4
    ac = m1 * m3 - m2 * m2
    bb = m0 * m4 - m2 * m2
    bc = m1 * m2 - m0 * m3
    cc = m0 * m2 - m1 * m1
    determ = m0 * aa + m1 * ab + m2 * ac
    aa, ab, ac, bb, bc, cc = (entry / determ for entry in (aa, ab, ac, bb, bc, cc))
    return ((aa, ab, ac), (ab, bb, bc), (ac, bc, cc))


def body(
    res_hbm, index_ref, table_ref, grid_hbm, high_ref, low_ref, tre_ref, tim_ref,
    comp_ref, spec_ref,
    grid_buf, res_buf, send_buf, recv_buf, core_send, own_buf, core_recv, z_recv, x_send, x_recv,
    grid_sem, res_sem, a_send, a_recv, c_send, c_recv, z_send_sem, z_recv_sem, x_send_sem, x_recv_sem,
):
    groups = lax.axis_size("chan")
    bands = lax.axis_size("band")
    zs = groups // 4
    chan = lax.axis_index("chan")
    band = lax.axis_index("band")
    x_lo = chan // (2 * zs)
    z_at = (chan // 2) % zs
    core = chan % 2
    count = res_hbm.shape[0]
    rows = res_hbm.shape[1]
    columns = res_hbm.shape[2] // groups
    row_tiles = rows // 8
    lane_tiles = columns // 128
    plane = row_tiles * lane_tiles
    blocks = grid_hbm.shape[1]
    pieces = send_buf.shape[1]
    halves = pieces // 2

    def chan_of(x, z, c):
        return (x * zs + z) * 2 + c

    def z_of(shift):
        return lax.rem(z_at + shift, zs)

    partner = {"chan": chan_of(x_lo, z_at, 1 - core)}
    across = {"chan": chan_of(1 - x_lo, z_at, core)}

    barrier = pltpu.get_barrier_semaphore()
    for shift in range(1, bands):
        pl.semaphore_signal(barrier, 1, device_id={"band": lax.rem(band + shift, bands)}, device_id_type=MESH)
    for shift in SHIFTS[:-1]:
        pl.semaphore_signal(barrier, 1, device_id={"chan": chan_of(x_lo, z_of(shift), core)}, device_id_type=MESH)
    pl.semaphore_signal(barrier, 1, device_id=partner, device_id_type=MESH)
    pl.semaphore_signal(barrier, 1, device_id=across, device_id_type=MESH)

    grid_copies = [
        pltpu.make_async_copy(grid_hbm.at[:, k], grid_buf.at[:, k], grid_sem.at[k]) for k in range(blocks)
    ]
    for copy in grid_copies:
        copy.start()
    slots = [(other, shift) for other in (1, 0) for shift in SHIFTS]
    order = [(away, slot) for away in (1, 0) for slot in range(len(slots))]

    def block_of(away, slot):
        other, shift = slots[slot]
        return chan_of((x_lo + other) % 2, z_of(shift), (core + away) % 2)

    res_copies = []
    for k, (away, slot) in enumerate(order):
        start = pl.multiple_of(block_of(away, slot) * columns, columns)
        res_copies.append(
            pltpu.make_async_copy(res_hbm.at[:, :, pl.ds(start, columns)], res_buf.at[k], res_sem.at[k])
        )
    for copy in res_copies:
        copy.start()

    for block in range(blocks):
        grid_copies[block].wait()

        def pair(step, carry, block=block):
            def taken(part, row):
                return grid_buf[part, block, pl.ds(row, RADIX, stride=8), :]

            first = step * 2
            value = jnp.concatenate(
                [
                    jnp.concatenate([taken(0, first), taken(0, first + 1)], axis=1),
                    jnp.concatenate([taken(1, first), taken(1, first + 1)], axis=1),
                ],
                axis=0,
            )
            high, low = (high_ref[...], low_ref[...])
            stage = three_products(high, low, value, ((1,), (0,)))
            real, imag = (stage[:RADIX], stage[RADIX:])
            tre, tim = (tre_ref[...], tim_ref[...])
            turned_re = real * tre - imag * tim
            turned_im = real * tim + imag * tre
            turned = jnp.concatenate(
                [
                    jnp.concatenate([turned_re[:, :RADIX], turned_im[:, :RADIX]], axis=1),
                    jnp.concatenate([turned_re[:, RADIX:], turned_im[:, RADIX:]], axis=1),
                ],
                axis=0,
            )
            final = three_products(high, low, turned, ((1,), (1,)))
            for half_row in range(2):
                row = block * 8 + first + half_row
                for target in range(bands):
                    for part in range(2):
                        for half in range(halves):
                            at = part * RADIX + target * (8 * halves) + half * 8
                            start = pl.multiple_of(row * 8, 8)
                            send_buf[target, half * 2 + part, pl.ds(start, 8), :] = final[
                                at : at + 8, half_row * RADIX : (half_row + 1) * RADIX
                            ]
            return carry

        lax.fori_loop(0, 4, pair, 0)

    peers = 7 + len(SHIFTS) - 1 + 2
    pl.semaphore_wait(barrier, peers)

    def spectrum_copy(piece, shift):
        target = lax.rem(band + shift, bands)
        at = piece * bands + shift
        return pltpu.make_async_remote_copy(
            src_ref=send_buf.at[target, piece],
            dst_ref=recv_buf.at[piece, band],
            send_sem=a_send.at[at],
            recv_sem=a_recv.at[at],
            device_id={"band": target},
            device_id_type=MESH,
        )

    spectrum_copies = [[spectrum_copy(piece, shift) for shift in range(1, bands)] for piece in range(pieces)]
    for piece in range(pieces):
        for copy in spectrum_copies[piece]:
            copy.start()

    weights, offsets = ([], [])
    for k in range(count):
        weights.append(table_ref[index_ref[k]])
        position = (chan * count + k).astype(jnp.float32)
        offsets.append((2.0 * position + 1.0) / (count * groups) - 1.0)
    coeffs = [weights, [w * o for w, o in zip(weights, offsets)], [w * o * o for w, o in zip(weights, offsets)]]
    powers = list(weights)
    moments = []
    for power in range(5):
        total = powers[0]
        for k in range(1, count):
            total = total + powers[k]
        moments.append(total)
        powers = [p * o for p, o in zip(powers, offsets)]
    sublane = lax.broadcasted_iota(jnp.int32, (8, 128), 0)
    moment_tile = jnp.zeros((8, 128), jnp.float32)
    for power in range(5):
        moment_tile = jnp.where(sublane == power, moments[power], moment_tile)

    def sums(k, target_ref, slot, extra):
        res_copies[k].wait()

        def tile(step, carry):
            row = step // lane_tiles
            lane = lax.rem(step, lane_tiles)
            rows_at = pl.ds(pl.multiple_of(row * 8, 8), 8)
            lanes_at = pl.ds(pl.multiple_of(lane * 128, 128), 128)
            totals = [None] * TERMS
            for channel in range(count):
                value = res_buf[k, channel, rows_at, lanes_at]
                for term in range(TERMS):
                    product = value * coeffs[term][channel]
                    totals[term] = product if totals[term] is None else totals[term] + product
            for term in range(TERMS):
                at = term * plane + step
                total = totals[term]
                if extra is not None:
                    total = total + extra[slot, at]
                target_ref[slot, at] = total
            return carry

        lax.fori_loop(0, plane, tile, 0, unroll=4)
        moment = moment_tile
        if extra is not None:
            moment = moment + extra[slot, TERMS * plane]
        target_ref[slot, TERMS * plane] = moment

    core_copies = []
    for slot in range(len(slots)):
        sums(slot, core_send, slot, None)
        copy = pltpu.make_async_remote_copy(
            src_ref=core_send.at[slot],
            dst_ref=core_recv.at[slot],
            send_sem=c_send.at[slot],
            recv_sem=c_recv.at[slot],
            device_id=partner,
            device_id_type=MESH,
        )
        copy.start()
        core_copies.append(copy)

    z_copies = {}
    for slot, (other, shift) in enumerate(slots):
        core_copies[slot].wait_recv()
        sums(len(slots) + slot, own_buf, slot, core_recv)
        if shift:
            copy = pltpu.make_async_remote_copy(
                src_ref=own_buf.at[slot],
                dst_ref=z_recv.at[slot],
                send_sem=z_send_sem.at[slot],
                recv_sem=z_recv_sem.at[slot],
                device_id={"chan": chan_of(x_lo, z_of(shift), core)},
                device_id_type=MESH,
            )
            copy.start()
            z_copies[slot] = copy

    own = send_buf.at[band]
    for piece in range(pieces):
        recv_buf[piece, band] = own[piece]

    def gathered(other, target):
        base = [k for k, key in enumerate(slots) if key == (other, 0)][0]
        came = [k for k, key in enumerate(slots) if key[0] == other and key[1]]
        for slot in came:
            z_copies[slot].wait_recv()

        def tile(step, carry):
            total = own_buf[base, step]
            for slot in came:
                total = total + z_recv[slot, step]
            target[step] = total
            return carry

        lax.fori_loop(0, TERMS * plane + 1, tile, 0)

    gathered(1, x_send)
    x_copy = pltpu.make_async_remote_copy(
        src_ref=x_send,
        dst_ref=x_recv,
        send_sem=x_send_sem,
        recv_sem=x_recv_sem,
        device_id=across,
        device_id_type=MESH,
    )
    x_copy.start()

    def place(piece):
        half, part = divmod(piece, 2)
        for copy in spectrum_copies[piece]:
            copy.wait_recv()

        def turn(k, carry):
            for side in range(2):
                value = jnp.concatenate(
                    [recv_buf[piece, side * 4 + source, pl.ds(k, 32, stride=8), :] for source in range(4)],
                    axis=0,
                )
                start = pl.multiple_of((half * 8 + k) * RADIX, RADIX)
                spec_ref[part, pl.ds(start, RADIX), pl.ds(side * 128, 128)] = value.T
            return carry

        lax.fori_loop(0, 8, turn, 0)

    def finish():
        gathered(0, own_buf.at[len(slots) - 1])
        x_copy.wait_recv()
        last = len(slots) - 1
        total = own_buf[last, TERMS * plane] + x_recv[TERMS * plane]
        inverse = solve_rows([total[k : k + 1] for k in range(5)], None)

        def tile(step, carry):
            row = step // lane_tiles
            lane = lax.rem(step, lane_tiles)
            rows_at = pl.ds(pl.multiple_of(row * 8, 8), 8)
            lanes_at = pl.ds(pl.multiple_of(lane * 128, 128), 128)
            taylor = [own_buf[last, s * plane + step] + x_recv[s * plane + step] for s in range(TERMS)]
            for t in range(TERMS):
                comp_ref[t, rows_at, lanes_at] = (
                    inverse[t][0] * taylor[0] + inverse[t][1] * taylor[1] + inverse[t][2] * taylor[2]
                )
            return carry

        lax.fori_loop(0, plane, tile, 0)

    for piece in range(pieces - 1):
        place(piece)
    finish()
    place(pieces - 1)

    for piece in range(pieces):
        for copy in spectrum_copies[piece]:
            copy.wait_send()
    for copy in core_copies:
        copy.wait_send()
    for copy in z_copies.values():
        copy.wait_send()
    x_copy.wait_send()


def local(residual, weight_index, weight_table, gridded):
    bands = lax.axis_size("band")
    groups = lax.axis_size("chan")
    count, rows, width = residual.shape
    grid_rows, length = gridded.shape[2:]
    blocks = grid_rows // 8
    tiled = gridded.reshape(2, blocks, 8, RADIX, RADIX)
    tiled = jnp.transpose(tiled, (0, 1, 3, 2, 4)).reshape(2, blocks, RADIX * 8, RADIX)
    columns = width // groups
    out_length = length // bands
    pieces = 2 * (RADIX // bands // 8)
    tiles = TERMS * (rows // 8) * (columns // 128) + 1
    f32 = jnp.float32
    any_space = pl.BlockSpec(memory_space=pl.ANY)
    vmem = pl.BlockSpec(memory_space=pltpu.VMEM)
    smem = pl.BlockSpec(memory_space=pltpu.SMEM)
    dma = pltpu.SemaphoreType.DMA
    slots = 2 * len(SHIFTS)
    components, spectrum = pl.pallas_call(
        body,
        out_shape=(
            pltpu.VMEM((TERMS, rows, columns), f32),
            pltpu.VMEM((2, out_length, grid_rows * bands), f32),
        ),
        in_specs=[any_space, smem, smem, any_space, vmem, vmem, vmem, vmem],
        out_specs=(vmem, vmem),
        scratch_shapes=[
            pltpu.VMEM((2, blocks, RADIX * 8, RADIX), f32),
            pltpu.VMEM((groups, count, rows, columns), f32),
            pltpu.VMEM((bands, pieces, grid_rows * 8, RADIX), f32),
            pltpu.VMEM((pieces, bands, grid_rows * 8, RADIX), f32),
            pltpu.VMEM((slots, tiles, 8, 128), f32),
            pltpu.VMEM((slots, tiles, 8, 128), f32),
            pltpu.VMEM((slots, tiles, 8, 128), f32),
            pltpu.VMEM((slots, tiles, 8, 128), f32),
            pltpu.VMEM((tiles, 8, 128), f32),
            pltpu.VMEM((tiles, 8, 128), f32),
            dma((blocks,)),
            dma((groups,)),
            dma((pieces * bands,)),
            dma((pieces * bands,)),
            dma((slots,)),
            dma((slots,)),
            dma((slots,)),
            dma((slots,)),
            dma,
            dma,
        ],
        compiler_params=pltpu.CompilerParams(
            collective_id=0, has_side_effects=True, vmem_limit_bytes=52 << 20
        ),
    )(residual, weight_index, weight_table, tiled, *(jnp.asarray(table) for table in tables()))
    return (components, spectrum.reshape(2, 1, out_length, grid_rows * bands))


def solution(mesh):
    in_specs = (P("chan", "band", None), P("chan"), P(), P(None, "chan", "band", None))
    out_specs = (P(None, "band", "chan"), P(None, "chan", "band", None))
    return jax.shard_map(local, mesh=mesh, in_specs=in_specs, out_specs=out_specs, check_vma=False)
```

profile of v0, /device:TPU:0, one launch (start us, length us, event | category | flops | bytes accessed | tf_op | source)
XLA Modules:
  0.0 76.2 jit_solution(17646212614365148423)
XLA Ops:
  0.6 72.8 %shard_map.95 = (f32[3,24,1024]{2,1,0:T(8,128)S(1)}, f32[2,2048,256]{2,1,0:T(8,128)S(1)}) custom-call(f32[8,24,16384]{2,1,0:T(8,128)} %res_hbm.1, s32[8]{0:T(128)} %index_ref.1, f32[16]{0:T(128)} %table_ref.1, f32[2,4,1024,128]{3,2,1,0:T(8,128)} %bitcast.9, bf16[256,256]{1,0:T(8,128)(2,1)} %constant.8.clone.high_ref, ...), custom_call_target="tpu_custom_call" | custom-call | tf_op jit(solution)/shard_map/pallas_call | solution.py:360
  73.4 0.7 copy.13
  74.2 2.0 %copy.14 = f32[2,1,2048,256]{3,2,1,0:T(8,128)} copy(f32[2,1,2048,256]{3,2,1,0:T(8,128)S(1)} %bitcast.8) | data formatting | bytes 8388608
where the time goes:
time: 77 us; the launch traced here: 76.2 us
  Pallas kernels  72.8 us (95%)
  local copies, waits for them, and re-layouts  2.73 us (4%)
    pallas_call x1, Pallas kernels, local(): pl.pallas_call(body, out_shape=(pltpu.VMEM((TERMS, rows, columns), f32),...  72.8 us
    unnamed x2, local copies, waits for them, and re-layouts  2.73 us

commit v1 on v0

--- a/solution.py
+++ b/solution.py
@@ -22,23 +22,26 @@
     high = whole.astype(jnp.bfloat16)
     low = (whole - high.astype(np.float32)).astype(jnp.bfloat16)
     turn = 2.0 * np.pi * np.outer(step, step) / (RADIX * RADIX)
-    twist_re = np.tile(np.cos(turn) / RADIX, (1, 2)).astype(np.float32)
-    twist_im = np.tile(-np.sin(turn) / RADIX, (1, 2)).astype(np.float32)
-    return (high, low, twist_re, twist_im)
-
-
-def split_pair(value):
-    high = value.astype(jnp.bfloat16)
-    low = (value - high.astype(jnp.float32)).astype(jnp.bfloat16)
-    return (high, low)
-
-
-def three_products(high, low, value, dims):
-    value_high, value_low = split_pair(value)
+    twist = np.stack([np.cos(turn), -np.sin(turn)]) / RADIX
+    return (np.concatenate([high, low]), twist.astype(np.float32))
+
+
+def three_products(pair, value, axis):
+    width = 2 * RADIX
     mul = functools.partial(
-        lax.dot_general, dimension_numbers=(dims, ((), ())), preferred_element_type=jnp.float32
+        lax.dot_general,
+        dimension_numbers=(((1,), (axis,)), ((), ())),
+        preferred_element_type=jnp.float32,
     )
-    return mul(high, value_high) + mul(high, value_low) + mul(low, value_high)
+    done = []
+    for k in range(value.shape[1 - axis] // width):
+        cut = slice(k * width, (k + 1) * width)
+        tile = value[:, cut] if axis == 0 else value[cut]
+        high = tile.astype(jnp.bfloat16)
+        low = (tile - high.astype(jnp.float32)).astype(jnp.bfloat16)
+        both = mul(pair, high)
+        done.append(both[:width] + (both[width:] + mul(pair[:width], low)))
+    return jnp.concatenate(done, axis=1)
 
 
 def solve_rows(moment, taylor):
@@ -55,10 +58,10 @@
 
 
 def body(
-    res_hbm, index_ref, table_ref, grid_hbm, high_ref, low_ref, tre_ref, tim_ref,
+    res_hbm, index_hbm, table_hbm, grid_hbm, pair_hbm, twist_hbm,
     comp_ref, spec_ref,
-    grid_buf, res_buf, send_buf, recv_buf, core_send, own_buf, core_recv, z_recv, x_send, x_recv,
-    grid_sem, res_sem, a_send, a_recv, c_send, c_recv, z_send_sem, z_recv_sem, x_send_sem, x_recv_sem,
+    index_ref, table_ref, pair_ref, twist_ref, grid_buf, res_buf, send_buf, recv_buf, core_send, own_buf, core_recv, z_recv, x_send, x_recv,
+    small_sem, grid_sem, res_sem, a_send, a_recv, c_send, c_recv, z_send_sem, z_recv_sem, x_send_sem, x_recv_sem,
 ):
     groups = lax.axis_size("chan")
     bands = lax.axis_size("band")
@@ -98,7 +101,13 @@
     grid_copies = [
         pltpu.make_async_copy(grid_hbm.at[:, k], grid_buf.at[:, k], grid_sem.at[k]) for k in range(blocks)
     ]
-    for copy in grid_copies:
+    small_copies = [
+        pltpu.make_async_copy(source, target, small_sem.at[k])
+        for k, (source, target) in enumerate(
+            ((pair_hbm, pair_ref), (twist_hbm, twist_ref), (index_hbm, index_ref), (table_hbm, table_ref))
+        )
+    ]
+    for copy in (grid_copies[0], *small_copies, *grid_copies[1:]):
         copy.start()
     slots = [(other, shift) for other in (1, 0) for shift in SHIFTS]
     order = [(away, slot) for away in (1, 0) for slot in range(len(slots))]
@@ -116,48 +125,36 @@
     for copy in res_copies:
         copy.start()
 
+    for copy in small_copies:
+        copy.wait()
+
+    def transform(block, carry):
+        def taken(part):
+            return jnp.concatenate([grid_buf[part, block, pl.ds(k, RADIX, stride=8), :] for k in range(8)], axis=1)
+
+        pair = pair_ref[...]
+        stage = three_products(pair, jnp.concatenate([taken(0), taken(1)], axis=0), 0)
+        tre, tim = (twist_ref[0], twist_ref[1])
+        turned = []
+        for k in range(8):
+            cut = slice(k * RADIX, (k + 1) * RADIX)
+            real, imag = (stage[:RADIX, cut], stage[RADIX:, cut])
+            turned.append(jnp.concatenate([real * tre - imag * tim, real * tim + imag * tre], axis=1))
+        final = three_products(pair, jnp.concatenate(turned, axis=0), 1)
+        for k in range(8):
+            start = pl.multiple_of(block * 64 + k * 8, 8)
+            for target in range(bands):
+                for part in range(2):
+                    for half in range(halves):
+                        at = part * RADIX + target * (8 * halves) + half * 8
+                        send_buf[target, half * 2 + part, pl.ds(start, 8), :] = final[
+                            at : at + 8, k * RADIX : (k + 1) * RADIX
+                        ]
+        return carry
+
     for block in range(blocks):
         grid_copies[block].wait()
-
-        def pair(step, carry, block=block):
-            def taken(part, row):
-                return grid_buf[part, block, pl.ds(row, RADIX, stride=8), :]
-
-            first = step * 2
-            value = jnp.concatenate(
-                [
-                    jnp.concatenate([taken(0, first), taken(0, first + 1)], axis=1),
-                    jnp.concatenate([taken(1, first), taken(1, first + 1)], axis=1),
-                ],
-                axis=0,
-            )
-            high, low = (high_ref[...], low_ref[...])
-            stage = three_products(high, low, value, ((1,), (0,)))
-            real, imag = (stage[:RADIX], stage[RADIX:])
-            tre, tim = (tre_ref[...], tim_ref[...])
-            turned_re = real * tre - imag * tim
-            turned_im = real * tim + imag * tre
-            turned = jnp.concatenate(
-                [
-                    jnp.concatenate([turned_re[:, :RADIX], turned_im[:, :RADIX]], axis=1),
-                    jnp.concatenate([turned_re[:, RADIX:], turned_im[:, RADIX:]], axis=1),
-                ],
-                axis=0,
-            )
-            final = three_products(high, low, turned, ((1,), (1,)))
-            for half_row in range(2):
-                row = block * 8 + first + half_row
-                for target in range(bands):
-                    for part in range(2):
-                        for half in range(halves):
-                            at = part * RADIX + target * (8 * halves) + half * 8
-                            start = pl.multiple_of(row * 8, 8)
-                            send_buf[target, half * 2 + part, pl.ds(start, 8), :] = final[
-                                at : at + 8, half_row * RADIX : (half_row + 1) * RADIX
-                            ]
-            return carry
-
-        lax.fori_loop(0, 4, pair, 0)
+        transform(block, 0)
 
     peers = 7 + len(SHIFTS) - 1 + 2
     pl.semaphore_wait(barrier, peers)
@@ -354,7 +351,6 @@
     f32 = jnp.float32
     any_space = pl.BlockSpec(memory_space=pl.ANY)
     vmem = pl.BlockSpec(memory_space=pltpu.VMEM)
-    smem = pl.BlockSpec(memory_space=pltpu.SMEM)
     dma = pltpu.SemaphoreType.DMA
     slots = 2 * len(SHIFTS)
     components, spectrum = pl.pallas_call(
@@ -363,9 +359,13 @@
             pltpu.VMEM((TERMS, rows, columns), f32),
             pltpu.VMEM((2, out_length, grid_rows * bands), f32),
         ),
-        in_specs=[any_space, smem, smem, any_space, vmem, vmem, vmem, vmem],
+        in_specs=[any_space] * 6,
         out_specs=(vmem, vmem),
         scratch_shapes=[
+            pltpu.SMEM(weight_index.shape, weight_index.dtype),
+            pltpu.SMEM(weight_table.shape, f32),
+            pltpu.VMEM((4 * RADIX, 2 * RADIX), jnp.bfloat16),
+            pltpu.VMEM((2, RADIX, RADIX), f32),
             pltpu.VMEM((2, blocks, RADIX * 8, RADIX), f32),
             pltpu.VMEM((groups, count, rows, columns), f32),
             pltpu.VMEM((bands, pieces, grid_rows * 8, RADIX), f32),
@@ -376,6 +376,7 @@
             pltpu.VMEM((slots, tiles, 8, 128), f32),
             pltpu.VMEM((tiles, 8, 128), f32),
             pltpu.VMEM((tiles, 8, 128), f32),
+            dma((4,)),
             dma((blocks,)),
             dma((groups,)),
             dma((pieces * bands,)),

time: 77 us -> 69.2 us (0.90)
  Pallas kernels: 72.8 us -> 65 us
    pallas_call x1, Pallas kernels: 72.8 us -> 65 us  [local(): pl.pallas_call(body, out_shape=(pltpu.VMEM((TERMS, rows, columns), f32),...]
where the time goes in v1:
time: 69.2 us; the launch traced here: 68.4 us
  Pallas kernels  65 us (94%)
  local copies, waits for them, and re-layouts  2.73 us (4%)
    pallas_call x1, Pallas kernels, local(): pl.pallas_call(body, out_shape=(pltpu.VMEM((TERMS, rows, columns), f32),...  65 us
    unnamed x2, local copies, waits for them, and re-layouts  2.73 us

profile of v1, /device:TPU:0, one launch (start us, length us, event | category | flops | bytes accessed | tf_op | source)
XLA Modules:
  0.0 68.4 jit_solution(7312946702094704088)
XLA Ops:
  0.6 65.0 %shard_map.77 = (f32[3,24,1024]{2,1,0:T(8,128)S(1)}, f32[2,2048,256]{2,1,0:T(8,128)S(1)}) custom-call(f32[8,24,16384]{2,1,0:T(8,128)} %res_hbm.1, s32[8]{0:T(128)} %index_hbm.1, f32[16]{0:T(128)} %table_hbm.1, f32[2,4,1024,128]{3,2,1,0:T(8,128)} %bitcast.9, bf16[512,256]{1,0:T(8,128)(2,1)} %constant.4.clone.pair_hbm, f32[2,128,128]{2,1,0:T(8,128)} %constant.5.clone.twist_hbm), custom_call_target="tpu_custom_call" | custom-call | tf_op jit(solution)/shard_map/pallas_call | solution.py:356
  65.6 0.7 %copy.11 = f32[3,24,1024]{2,1,0:T(8,128)} copy(f32[3,24,1024]{2,1,0:T(8,128)S(1)} %get-tuple-element.8) | data formatting | bytes 589824
  66.4 2.0 %copy.12 = f32[2,1,2048,256]{3,2,1,0:T(8,128)} copy(f32[2,1,2048,256]{3,2,1,0:T(8,128)S(1)} %bitcast.8) | data formatting | bytes 8388608

commit v2 on v1

--- a/solution.py
+++ b/solution.py
@@ -122,8 +122,6 @@
         res_copies.append(
             pltpu.make_async_copy(res_hbm.at[:, :, pl.ds(start, columns)], res_buf.at[k], res_sem.at[k])
         )
-    for copy in res_copies:
-        copy.start()
 
     for copy in small_copies:
         copy.wait()
@@ -154,6 +152,9 @@
 
     for block in range(blocks):
         grid_copies[block].wait()
+        if block == blocks - 1:
+            for copy in res_copies:
+                copy.start()
         transform(block, 0)
 
     peers = 7 + len(SHIFTS) - 1 + 2
@@ -321,10 +322,9 @@
 
         lax.fori_loop(0, plane, tile, 0)
 
-    for piece in range(pieces - 1):
+    for piece in range(pieces):
         place(piece)
     finish()
-    place(pieces - 1)
 
     for piece in range(pieces):
         for copy in spectrum_copies[piece]:
@@ -334,6 +334,15 @@
     for copy in z_copies.values():
         copy.wait_send()
     x_copy.wait_send()
+
+
+def write_out(comp_ref, spec_ref, comp_hbm, spec_hbm, sem):
+    copies = [pltpu.make_async_copy(comp_ref, comp_hbm, sem.at[0])]
+    copies += [pltpu.make_async_copy(spec_ref.at[part], spec_hbm.at[part], sem.at[1 + part]) for part in range(2)]
+    for copy in copies:
+        copy.start()
+    for copy in copies:
+        copy.wait()
 
 
 def local(residual, weight_index, weight_table, gridded):
@@ -392,6 +401,17 @@
             collective_id=0, has_side_effects=True, vmem_limit_bytes=52 << 20
         ),
     )(residual, weight_index, weight_table, tiled, *(jnp.asarray(table) for table in tables()))
+    components, spectrum = pl.pallas_call(
+        write_out,
+        out_shape=(
+            jax.ShapeDtypeStruct(components.shape, f32),
+            jax.ShapeDtypeStruct(spectrum.shape, f32),
+        ),
+        in_specs=[vmem, vmem],
+        out_specs=(any_space, any_space),
+        scratch_shapes=[dma((3,))],
+        compiler_params=pltpu.CompilerParams(vmem_limit_bytes=6 << 20),
+    )(*(pltpu.with_memory_space_constraint(array, pltpu.VMEM) for array in (components, spectrum)))
     return (components, spectrum.reshape(2, 1, out_length, grid_rows * bands))
 
 

time: 69.2 us -> 64.7 us (0.935)
  local copies, waits for them, and re-layouts: 2.73 us -> 0 us
  Pallas kernels: 65 us -> 63.3 us
    pallas_call x1, Pallas kernels: 65 us -> 61.2 us  [local(): pl.pallas_call(body, out_shape=(pltpu.VMEM((TERMS, rows, columns), f32),...]
    unnamed x2 -> x0, local copies, waits for them, and re-layouts: 2.73 us -> none
    pallas_call x0 -> x1, Pallas kernels: none -> 2.13 us  [local(): pl.pallas_call(write_out, out_shape=(jax.ShapeDtypeStruct(components.shap...]
where the time goes in v2:
time: 64.7 us; the launch traced here: 63.9 us
  Pallas kernels  63.3 us (98%)
    pallas_call x1, Pallas kernels, local(): pl.pallas_call(body, out_shape=(pltpu.VMEM((TERMS, rows, columns), f32),...  61.2 us
    pallas_call x1, Pallas kernels, local(): pl.pallas_call(write_out, out_shape=(jax.ShapeDtypeStruct(components.shap...  2.13 us

profile of v2, /device:TPU:0, one launch (start us, length us, event | category | flops | bytes accessed | tf_op | source)
XLA Modules:
  0.0 63.9 jit_solution(10019253136384010220)
XLA Ops:
  0.6 61.2 %shard_map.77 = (f32[3,24,1024]{2,1,0:T(8,128)S(1)}, f32[2,2048,256]{2,1,0:T(8,128)S(1)}) custom-call(f32[8,24,16384]{2,1,0:T(8,128)} %res_hbm.1, s32[8]{0:T(128)} %index_hbm.1, f32[16]{0:T(128)} %table_hbm.1, f32[2,4,1024,128]{3,2,1,0:T(8,128)} %bitcast.8, bf16[512,256]{1,0:T(8,128)(2,1)} %constant.4.clone.pair_hbm, f32[2,128,128]{2,1,0:T(8,128)} %constant.5.clone.twist_hbm), custom_call_target="tpu_custom_call" | custom-call | tf_op jit(solution)/shard_map/pallas_call | solution.py:365
  61.8 2.1 %shard_map.78 = (f32[3,24,1024]{2,1,0:T(8,128)}, f32[2,2048,256]{2,1,0:T(8,128)}) custom-call(f32[3,24,1024]{2,1,0:T(8,128)S(1)} %get-tuple-element.6.comp_ref, f32[2,2048,256]{2,1,0:T(8,128)S(1)} %get-tuple-element.7.spec_ref), custom_call_target="tpu_custom_call" | custom-call | tf_op jit(solution)/shard_map/pallas_call | solution.py:404

commit v3 on v2

--- a/solution.py
+++ b/solution.py
@@ -12,6 +12,7 @@
 RADIX = 128
 TERMS = 3
 SHIFTS = (2, 1, 3, 0)
+READY = 1
 
 
 def tables():
@@ -78,8 +79,7 @@
     lane_tiles = columns // 128
     plane = row_tiles * lane_tiles
     blocks = grid_hbm.shape[1]
-    pieces = send_buf.shape[1]
-    halves = pieces // 2
+    halves = send_buf.shape[2] // 2
 
     def chan_of(x, z, c):
         return (x * zs + z) * 2 + c
@@ -126,7 +126,7 @@
     for copy in small_copies:
         copy.wait()
 
-    def transform(block, carry):
+    def transform(block):
         def taken(part):
             return jnp.concatenate([grid_buf[part, block, pl.ds(k, RADIX, stride=8), :] for k in range(8)], axis=1)
 
@@ -140,25 +140,13 @@
             turned.append(jnp.concatenate([real * tre - imag * tim, real * tim + imag * tre], axis=1))
         final = three_products(pair, jnp.concatenate(turned, axis=0), 1)
         for k in range(8):
-            start = pl.multiple_of(block * 64 + k * 8, 8)
             for target in range(bands):
                 for part in range(2):
                     for half in range(halves):
                         at = part * RADIX + target * (8 * halves) + half * 8
-                        send_buf[target, half * 2 + part, pl.ds(start, 8), :] = final[
+                        send_buf[target, block, half * 2 + part, k * 8 : k * 8 + 8, :] = final[
                             at : at + 8, k * RADIX : (k + 1) * RADIX
                         ]
-        return carry
-
-    for block in range(blocks):
-        grid_copies[block].wait()
-        if block == blocks - 1:
-            for copy in res_copies:
-                copy.start()
-        transform(block, 0)
-
-    peers = 7 + len(SHIFTS) - 1 + 2
-    pl.semaphore_wait(barrier, peers)
 
     def spectrum_copy(piece, shift):
         target = lax.rem(band + shift, bands)
@@ -172,10 +160,22 @@
             device_id_type=MESH,
         )
 
-    spectrum_copies = [[spectrum_copy(piece, shift) for shift in range(1, bands)] for piece in range(pieces)]
-    for piece in range(pieces):
-        for copy in spectrum_copies[piece]:
-            copy.start()
+    spectrum_copies = [[spectrum_copy(piece, shift) for shift in range(1, bands)] for piece in range(blocks)]
+    peers = bands - 1 + len(SHIFTS) - 1 + 2
+    for block in range(blocks):
+        grid_copies[block].wait()
+        if block == blocks - 1:
+            for copy in res_copies:
+                copy.start()
+        transform(block)
+        if block == READY:
+            pl.semaphore_wait(barrier, peers)
+            for piece in range(READY):
+                for copy in spectrum_copies[piece]:
+                    copy.start()
+        if block >= READY:
+            for copy in spectrum_copies[block]:
+                copy.start()
 
     weights, offsets = ([], [])
     for k in range(count):
@@ -255,7 +255,7 @@
             z_copies[slot] = copy
 
     own = send_buf.at[band]
-    for piece in range(pieces):
+    for piece in range(blocks):
         recv_buf[piece, band] = own[piece]
 
     def gathered(other, target):
@@ -284,15 +284,15 @@
     )
     x_copy.start()
 
-    def place(piece):
-        half, part = divmod(piece, 2)
-        for copy in spectrum_copies[piece]:
-            copy.wait_recv()
-
+    def place(half, part):
         def turn(k, carry):
             for side in range(2):
                 value = jnp.concatenate(
-                    [recv_buf[piece, side * 4 + source, pl.ds(k, 32, stride=8), :] for source in range(4)],
+                    [
+                        recv_buf[piece, side * 4 + source, half * 2 + part, pl.ds(k, 8, stride=8), :]
+                        for source in range(4)
+                        for piece in range(blocks)
+                    ],
                     axis=0,
                 )
                 start = pl.multiple_of((half * 8 + k) * RADIX, RADIX)
@@ -322,12 +322,16 @@
 
         lax.fori_loop(0, plane, tile, 0)
 
-    for piece in range(pieces):
-        place(piece)
+    for copies in spectrum_copies:
+        for copy in copies:
+            copy.wait_recv()
+    for half in range(halves):
+        for part in range(2):
+            place(half, part)
     finish()
 
-    for piece in range(pieces):
-        for copy in spectrum_copies[piece]:
+    for copies in spectrum_copies:
+        for copy in copies:
             copy.wait_send()
     for copy in core_copies:
         copy.wait_send()
@@ -355,7 +359,7 @@
     tiled = jnp.transpose(tiled, (0, 1, 3, 2, 4)).reshape(2, blocks, RADIX * 8, RADIX)
     columns = width // groups
     out_length = length // bands
-    pieces = 2 * (RADIX // bands // 8)
+    quarters = 2 * (RADIX // bands // 8)
     tiles = TERMS * (rows // 8) * (columns // 128) + 1
     f32 = jnp.float32
     any_space = pl.BlockSpec(memory_space=pl.ANY)
@@ -377,8 +381,8 @@
             pltpu.VMEM((2, RADIX, RADIX), f32),
             pltpu.VMEM((2, blocks, RADIX * 8, RADIX), f32),
             pltpu.VMEM((groups, count, rows, columns), f32),
-            pltpu.VMEM((bands, pieces, grid_rows * 8, RADIX), f32),
-            pltpu.VMEM((pieces, bands, grid_rows * 8, RADIX), f32),
+            pltpu.VMEM((bands, blocks, quarters, 64, RADIX), f32),
+            pltpu.VMEM((blocks, bands, quarters, 64, RADIX), f32),
             pltpu.VMEM((slots, tiles, 8, 128), f32),
             pltpu.VMEM((slots, tiles, 8, 128), f32),
             pltpu.VMEM((slots, tiles, 8, 128), f32),
@@ -388,8 +392,8 @@
             dma((4,)),
             dma((blocks,)),
             dma((groups,)),
-            dma((pieces * bands,)),
-            dma((pieces * bands,)),
+            dma((blocks * bands,)),
+            dma((blocks * bands,)),
             dma((slots,)),
             dma((slots,)),
             dma((slots,)),

time: 64.7 us -> 62.7 us (0.969)
  Pallas kernels: 63.3 us -> 61.9 us
    pallas_call x1, Pallas kernels: 61.2 us -> 59.8 us  [local(): pl.pallas_call(body, out_shape=(pltpu.VMEM((TERMS, rows, columns), f32),...]
where the time goes in v3:
time: 62.7 us; the launch traced here: 62.6 us
  Pallas kernels  61.9 us (99%)
  between operations  0.64 us (1%)
    pallas_call x1, Pallas kernels, local(): pl.pallas_call(body, out_shape=(pltpu.VMEM((TERMS, rows, columns), f32),...  59.8 us
    pallas_call x1, Pallas kernels, local(): pl.pallas_call(write_out, out_shape=(jax.ShapeDtypeStruct(components.shap...  2.13 us

profile of v3, /device:TPU:0, one launch (start us, length us, event | category | flops | bytes accessed | tf_op | source)
XLA Modules:
  0.0 62.6 jit_solution(15593481404429426707)
XLA Ops:
  0.6 59.8 %shard_map.77 = (f32[3,24,1024]{2,1,0:T(8,128)S(1)}, f32[2,2048,256]{2,1,0:T(8,128)S(1)}) custom-call(f32[8,24,16384]{2,1,0:T(8,128)} %res_hbm.1, s32[8]{0:T(128)} %index_hbm.1, f32[16]{0:T(128)} %table_hbm.1, f32[2,4,1024,128]{3,2,1,0:T(8,128)} %bitcast.8, bf16[512,256]{1,0:T(8,128)(2,1)} %constant.4.clone.pair_hbm, f32[2,128,128]{2,1,0:T(8,128)} %constant.5.clone.twist_hbm), custom_call_target="tpu_custom_call" | custom-call | tf_op jit(solution)/shard_map/pallas_call | solution.py:369
  60.4 2.1 %shard_map.78 = (f32[3,24,1024]{2,1,0:T(8,128)}, f32[2,2048,256]{2,1,0:T(8,128)}) custom-call(f32[3,24,1024]{2,1,0:T(8,128)S(1)} %get-tuple-element.6.comp_ref, f32[2,2048,256]{2,1,0:T(8,128)S(1)} %get-tuple-element.7.spec_ref), custom_call_target="tpu_custom_call" | custom-call | tf_op jit(solution)/shard_map/pallas_call | solution.py:408

commit v4 on v3

--- a/solution.py
+++ b/solution.py
@@ -13,6 +13,7 @@
 TERMS = 3
 SHIFTS = (2, 1, 3, 0)
 READY = 1
+FAR = 2
 
 
 def tables():
@@ -62,7 +63,7 @@
     res_hbm, index_hbm, table_hbm, grid_hbm, pair_hbm, twist_hbm,
     comp_ref, spec_ref,
     index_ref, table_ref, pair_ref, twist_ref, grid_buf, res_buf, send_buf, recv_buf, core_send, own_buf, core_recv, z_recv, x_send, x_recv,
-    small_sem, grid_sem, res_sem, a_send, a_recv, c_send, c_recv, z_send_sem, z_recv_sem, x_send_sem, x_recv_sem,
+    word_sem, small_sem, grid_sem, res_sem, a_send, a_recv, c_send, c_recv, z_send_sem, z_recv_sem, x_send_sem, x_recv_sem,
 ):
     groups = lax.axis_size("chan")
     bands = lax.axis_size("band")
@@ -72,6 +73,9 @@
     x_lo = chan // (2 * zs)
     z_at = (chan // 2) % zs
     core = chan % 2
+    ys = bands // 2
+    y_at = band // 2
+    x_hi = band % 2
     count = res_hbm.shape[0]
     rows = res_hbm.shape[1]
     columns = res_hbm.shape[2] // groups
@@ -90,13 +94,19 @@
     partner = {"chan": chan_of(x_lo, z_at, 1 - core)}
     across = {"chan": chan_of(1 - x_lo, z_at, core)}
 
+    def along(turn):
+        return {"band": lax.rem(y_at + turn, ys) * 2 + x_hi}
+
+    def beyond(turn):
+        return {"band": lax.rem(y_at + turn, ys) * 2 + 1 - x_hi}
+
+    def up(turn):
+        return {"chan": chan_of(x_lo, z_of(turn), core)}
+
+    nearest = (beyond(0), along(1), along(ys - 1), up(1), up(zs - 1), partner, across)
     barrier = pltpu.get_barrier_semaphore()
-    for shift in range(1, bands):
-        pl.semaphore_signal(barrier, 1, device_id={"band": lax.rem(band + shift, bands)}, device_id_type=MESH)
-    for shift in SHIFTS[:-1]:
-        pl.semaphore_signal(barrier, 1, device_id={"chan": chan_of(x_lo, z_of(shift), core)}, device_id_type=MESH)
-    pl.semaphore_signal(barrier, 1, device_id=partner, device_id_type=MESH)
-    pl.semaphore_signal(barrier, 1, device_id=across, device_id_type=MESH)
+    for device in nearest:
+        pl.semaphore_signal(barrier, 1, device_id=device, device_id_type=MESH)
 
     grid_copies = [
         pltpu.make_async_copy(grid_hbm.at[:, k], grid_buf.at[:, k], grid_sem.at[k]) for k in range(blocks)
@@ -148,20 +158,26 @@
                             at : at + 8, k * RADIX : (k + 1) * RADIX
                         ]
 
-    def spectrum_copy(piece, shift):
-        target = lax.rem(band + shift, bands)
-        at = piece * bands + shift
+    def spectrum_copy(piece, crossing, turn):
+        device = beyond(turn) if crossing else along(turn)
+        at = piece * bands + turn * 2 + crossing
         return pltpu.make_async_remote_copy(
-            src_ref=send_buf.at[target, piece],
+            src_ref=send_buf.at[device["band"], piece],
             dst_ref=recv_buf.at[piece, band],
             send_sem=a_send.at[at],
             recv_sem=a_recv.at[at],
-            device_id={"band": target},
+            device_id=device,
             device_id_type=MESH,
         )
 
-    spectrum_copies = [[spectrum_copy(piece, shift) for shift in range(1, bands)] for piece in range(blocks)]
-    peers = bands - 1 + len(SHIFTS) - 1 + 2
+    ways = [(1, 2), (1, 1), (1, ys - 1), (0, 2), (1, 0), (0, 1), (0, ys - 1)]
+    spectrum_copies = [[spectrum_copy(piece, *way) for way in ways] for piece in range(blocks)]
+
+    def started(pieces, chosen):
+        for piece in pieces:
+            for way in chosen:
+                spectrum_copies[piece][way].start()
+
     for block in range(blocks):
         grid_copies[block].wait()
         if block == blocks - 1:
@@ -169,13 +185,23 @@
                 copy.start()
         transform(block)
         if block == READY:
-            pl.semaphore_wait(barrier, peers)
-            for piece in range(READY):
-                for copy in spectrum_copies[piece]:
-                    copy.start()
-        if block >= READY:
-            for copy in spectrum_copies[block]:
-                copy.start()
+            pl.semaphore_wait(barrier, len(nearest))
+            pl.semaphore_signal(word_sem.at[0], 1, device_id=beyond(0), device_id_type=MESH)
+            pl.semaphore_signal(word_sem.at[1], 1, device_id=along(ys - 1), device_id_type=MESH)
+            pl.semaphore_signal(word_sem.at[2], 1, device_id=up(zs - 1), device_id_type=MESH)
+            started(range(READY + 1), (4,))
+            started((0,), (5, 6))
+        if block == FAR:
+            pl.semaphore_wait(word_sem.at[1], 1)
+            pl.semaphore_signal(word_sem.at[3], 1, device_id=beyond(0), device_id_type=MESH)
+            pl.semaphore_wait(word_sem.at[0], 1)
+            started((0,), (1, 2, 3))
+            started(range(1, READY + 1), (1, 2, 3, 5, 6))
+        if block == blocks - 1:
+            pl.semaphore_wait(word_sem.at[3], 1)
+            pl.semaphore_wait(word_sem.at[2], 1)
+            started(range(READY + 1), (0,))
+            started(range(READY + 1, blocks), range(7))
 
     weights, offsets = ([], [])
     for k in range(count):
@@ -389,6 +415,7 @@
             pltpu.VMEM((slots, tiles, 8, 128), f32),
             pltpu.VMEM((tiles, 8, 128), f32),
             pltpu.VMEM((tiles, 8, 128), f32),
+            pltpu.SemaphoreType.REGULAR((4,)),
             dma((4,)),
             dma((blocks,)),
             dma((groups,)),

time: 62.7 us -> 61.9 us (0.987)
  Pallas kernels: 61.9 us -> 61.2 us
    pallas_call x1, Pallas kernels: 59.8 us -> 59 us  [local(): pl.pallas_call(body, out_shape=(pltpu.VMEM((TERMS, rows, columns), f32),...]
where the time goes in v4:
time: 61.9 us; the launch traced here: 61.8 us
  Pallas kernels  61.2 us (99%)
  between operations  0.64 us (1%)
    pallas_call x1, Pallas kernels, local(): pl.pallas_call(body, out_shape=(pltpu.VMEM((TERMS, rows, columns), f32),...  59 us
    pallas_call x1, Pallas kernels, local(): pl.pallas_call(write_out, out_shape=(jax.ShapeDtypeStruct(components.shap...  2.13 us

profile of v4, /device:TPU:0, one launch (start us, length us, event | category | flops | bytes accessed | tf_op | source)
XLA Modules:
  0.0 61.8 jit_solution(16559309659036948070)
XLA Ops:
  0.6 59.0 %shard_map.77 = (f32[3,24,1024]{2,1,0:T(8,128)S(1)}, f32[2,2048,256]{2,1,0:T(8,128)S(1)}) custom-call(f32[8,24,16384]{2,1,0:T(8,128)} %res_hbm.1, s32[8]{0:T(128)} %index_hbm.1, f32[16]{0:T(128)} %table_hbm.1, f32[2,4,1024,128]{3,2,1,0:T(8,128)} %bitcast.8, bf16[512,256]{1,0:T(8,128)(2,1)} %constant.4.clone.pair_hbm, f32[2,128,128]{2,1,0:T(8,128)} %constant.5.clone.twist_hbm), custom_call_target="tpu_custom_call" | custom-call | tf_op jit(solution)/shard_map/pallas_call | solution.py:395
  59.7 2.1 %shard_map.78 = (f32[3,24,1024]{2,1,0:T(8,128)}, f32[2,2048,256]{2,1,0:T(8,128)}) custom-call(f32[3,24,1024]{2,1,0:T(8,128)S(1)} %get-tuple-element.6.comp_ref, f32[2,2048,256]{2,1,0:T(8,128)S(1)} %get-tuple-element.7.spec_ref), custom_call_target="tpu_custom_call" | custom-call | tf_op jit(solution)/shard_map/pallas_call | solution.py:435

commit v5 on v4

--- a/solution.py
+++ b/solution.py
@@ -158,12 +158,12 @@
                             at : at + 8, k * RADIX : (k + 1) * RADIX
                         ]
 
-    def spectrum_copy(piece, crossing, turn):
+    def spectrum_copy(piece, length, crossing, turn):
         device = beyond(turn) if crossing else along(turn)
         at = piece * bands + turn * 2 + crossing
         return pltpu.make_async_remote_copy(
-            src_ref=send_buf.at[device["band"], piece],
-            dst_ref=recv_buf.at[piece, band],
+            src_ref=send_buf.at[device["band"], pl.ds(piece, length)],
+            dst_ref=recv_buf.at[band, pl.ds(piece, length)],
             send_sem=a_send.at[at],
             recv_sem=a_recv.at[at],
             device_id=device,
@@ -171,7 +171,10 @@
         )
 
     ways = [(1, 2), (1, 1), (1, ys - 1), (0, 2), (1, 0), (0, 1), (0, ys - 1)]
-    spectrum_copies = [[spectrum_copy(piece, *way) for way in ways] for piece in range(blocks)]
+    spectrum_copies = [
+        [spectrum_copy(piece, 1 if piece <= READY else blocks - 1 - READY, *way) for way in ways]
+        for piece in range(READY + 2)
+    ]
 
     def started(pieces, chosen):
         for piece in pieces:
@@ -201,7 +204,7 @@
             pl.semaphore_wait(word_sem.at[3], 1)
             pl.semaphore_wait(word_sem.at[2], 1)
             started(range(READY + 1), (0,))
-            started(range(READY + 1, blocks), range(7))
+            started((READY + 1,), range(7))
 
     weights, offsets = ([], [])
     for k in range(count):
@@ -282,7 +285,7 @@
 
     own = send_buf.at[band]
     for piece in range(blocks):
-        recv_buf[piece, band] = own[piece]
+        recv_buf[band, piece] = own[piece]
 
     def gathered(other, target):
         base = [k for k, key in enumerate(slots) if key == (other, 0)][0]
@@ -315,7 +318,7 @@
             for side in range(2):
                 value = jnp.concatenate(
                     [
-                        recv_buf[piece, side * 4 + source, half * 2 + part, pl.ds(k, 8, stride=8), :]
+                        recv_buf[side * 4 + source, piece, half * 2 + part, pl.ds(k, 8, stride=8), :]
                         for source in range(4)
                         for piece in range(blocks)
                     ],
@@ -408,7 +411,7 @@
             pltpu.VMEM((2, blocks, RADIX * 8, RADIX), f32),
             pltpu.VMEM((groups, count, rows, columns), f32),
             pltpu.VMEM((bands, blocks, quarters, 64, RADIX), f32),
-            pltpu.VMEM((blocks, bands, quarters, 64, RADIX), f32),
+            pltpu.VMEM((bands, blocks, quarters, 64, RADIX), f32),
             pltpu.VMEM((slots, tiles, 8, 128), f32),
             pltpu.VMEM((slots, tiles, 8, 128), f32),
             pltpu.VMEM((slots, tiles, 8, 128), f32),

time: 61.9 us -> 62.1 us (level)
  no operation moved by 1% of the time
where the time goes in v5:
time: 62.1 us; the launch traced here: 62 us
  Pallas kernels  61.4 us (99%)
  between operations  0.64 us (1%)
    pallas_call x1, Pallas kernels, local(): pl.pallas_call(body, out_shape=(pltpu.VMEM((TERMS, rows, columns), f32),...  59.2 us
    pallas_call x1, Pallas kernels, local(): pl.pallas_call(write_out, out_shape=(jax.ShapeDtypeStruct(components.shap...  2.13 us

profile of v5, /device:TPU:0, one launch (start us, length us, event | category | flops | bytes accessed | tf_op | source)
XLA Modules:
  0.0 62.0 jit_solution(5651391682890040036)
XLA Ops:
  0.6 59.2 %shard_map.77 = (f32[3,24,1024]{2,1,0:T(8,128)S(1)}, f32[2,2048,256]{2,1,0:T(8,128)S(1)}) custom-call(f32[8,24,16384]{2,1,0:T(8,128)} %res_hbm.1, s32[8]{0:T(128)} %index_hbm.1, f32[16]{0:T(128)} %table_hbm.1, f32[2,4,1024,128]{3,2,1,0:T(8,128)} %bitcast.8, bf16[512,256]{1,0:T(8,128)(2,1)} %constant.4.clone.pair_hbm, f32[2,128,128]{2,1,0:T(8,128)} %constant.5.clone.twist_hbm), custom_call_target="tpu_custom_call" | custom-call | tf_op jit(solution)/shard_map/pallas_call | solution.py:398
  59.9 2.1 %shard_map.78 = (f32[3,24,1024]{2,1,0:T(8,128)}, f32[2,2048,256]{2,1,0:T(8,128)}) custom-call(f32[3,24,1024]{2,1,0:T(8,128)S(1)} %get-tuple-element.6.comp_ref, f32[2,2048,256]{2,1,0:T(8,128)S(1)} %get-tuple-element.7.spec_ref), custom_call_target="tpu_custom_call" | custom-call | tf_op jit(solution)/shard_map/pallas_call | solution.py:438
